TPU v7x, 128 devices: a whole 4x4x4 slice. The times are simulated.
128 devices in a mesh: own: 32 (over x, z, core), rep: 4 (over y).
Axes of the slice: x: 4, y: 4, z: 4, core: 2. Of those that a mesh axis runs over, the one named last changes fastest.
Arguments:
- block_pool: bfloat16 [8192, 64, 576], P(('own', 'rep')), may hold values from -16 to 16
- sel_index: int32 [4096], P(('own', 'rep')), may hold values from 0 to 63
- sel_layer: int32 [4096], P(('own', 'rep')), may hold values from 0 to 15, as said below
- counts: int32 [128], P(('own', 'rep')), may hold values from 8 to 32, as said below
Outputs:
- quant_codes: bfloat16 [32, 4, 32, 8, 18432], P('own', 'rep')
- quant_steps: float32 [32, 288], P('own')
- clip_error: float32 [32, 288], P('own')
Inputs may be any that keep to these rules, and one draw needn't show every extreme that they name: `sel_layer`: among the 32 entries of one device, at most 8 name any one layer; the first 8 entries of every device all name one and the same layer. `counts`: some device has all 32 entries live.
All inputs are finite; a program needn't handle non-finite values.
Results may differ from a plain program's by a relative error of at most 0.001.
Values may be sent and summed in bfloat16 or wider, within the bound.
A program may use at most 128 MiB of HBM per device.

v0:
```python
import functools
import math

import jax
import jax.numpy as jnp
from jax import lax
from jax.experimental import pallas as pl
from jax.experimental.pallas import tpu as pltpu
from jax.sharding import PartitionSpec as P

SLICES = 2
LANES = 128
headroom = 0.5


def partner_layer(my_layer, layers, k):
    near = layers // 2
    if k < near:
        return lax.rem(my_layer + k, near) + (1 - my_layer // near) * near
    return lax.rem(my_layer + 1 + k - near, near) + (my_layer // near) * near


def send_order(layers):
    straight, across, both = range(1), range(1, SLICES), range(SLICES)
    own = [(layers - 1, across)]
    near = [(k, both) for k in range(layers // 2, layers - 1)]
    far = [(k, part) for k in range(1, layers // 2) for part in (across, straight)]
    return [(0, across), (0, straight)] + near + far + own


def fill_slots(live, index_row, layer_row, table, layers, cap, empty):
    n_select = index_row.shape[1]
    is_live = lax.broadcasted_iota(jnp.int32, (1, n_select), 1) < live
    before = lax.broadcasted_iota(jnp.int32, (n_select, n_select), 0)
    after = lax.broadcasted_iota(jnp.int32, (n_select, n_select), 1)
    earlier = jnp.where(before < after, 1.0, 0.0)
    wanted = lax.broadcasted_iota(jnp.int32, (layers, n_select), 0)
    matches = jnp.where((layer_row == wanted) & is_live, 1.0, 0.0)
    ranking = jnp.dot(matches, earlier, preferred_element_type=jnp.float32)
    slot = lax.broadcasted_iota(jnp.int32, (cap, n_select), 0).astype(jnp.float32)
    shifted = index_row.astype(jnp.float32) - float(empty)
    for layer in range(layers):
        hit = (ranking[layer:layer + 1] == slot) & (matches[layer:layer + 1] > 0.5)
        found = jnp.sum(jnp.where(hit, shifted, 0.0), axis=1, keepdims=True) + float(empty)
        table[layer * cap:(layer + 1) * cap, :] = jnp.broadcast_to(found, (cap, LANES)).astype(jnp.int32)


def kernel(own_n, rep_n, cap, live_ref, index_ref, layer_ref, pool_ref, codes_ref, steps_ref, err_ref,
           table, slots, pool_v, stage, send, recv, pk_send, pk_recv, pk_mine, pk_rep, er_mine, er_rep,
           table_sem, pool_sem, ssem, rsem, pssem, prsem, rpssem, rprsem, ressem, rersem):
    rows, tokens, width = pool_ref.shape
    half = width // SLICES
    flat = tokens * half
    group = LANES // math.gcd(half, LANES)
    period = group * half
    layers = own_n // SLICES
    me = lax.axis_index("own")
    rep = lax.axis_index("rep")
    my_layer = me // SLICES
    my_slice = me % SLICES
    tiles = stage.shape[0]
    denominator = float(own_n * rep_n * cap * tokens)
    pieces = pool_sem.shape[0]
    per_piece = rows // pieces

    loads = [
        pltpu.make_async_copy(
            pool_ref.at[pl.ds(p * per_piece, per_piece)],
            pool_v.at[pl.ds(p * per_piece, per_piece)],
            pool_sem.at[p],
        )
        for p in range(pieces)
    ]
    for load in loads:
        load.start()

    barrier = pltpu.get_barrier_semaphore()
    for k in range(1, own_n):
        pl.semaphore_signal(barrier, inc=1, device_id={"own": lax.rem(me + k, own_n)},
                            device_id_type=pl.DeviceIdType.MESH)
    for k in range(1, rep_n):
        pl.semaphore_signal(barrier, inc=1, device_id={"rep": lax.rem(rep + k, rep_n)},
                            device_id_type=pl.DeviceIdType.MESH)

    pool_v[rows] = jnp.zeros((tokens, width), pool_v.dtype)
    fill_slots(live_ref[0], index_ref[...], layer_ref[...], table, layers, cap, rows)
    to_scalars = pltpu.make_async_copy(table, slots, table_sem)
    to_scalars.start()
    to_scalars.wait()
    for load in loads:
        load.wait()

    def row_of(slot):
        return jnp.minimum(jnp.maximum(slots[slot, 0], 0), rows)

    def layer_peak(layer, carry):
        best = jnp.zeros((tokens, width), pool_v.dtype)
        for c in range(cap):
            best = jnp.maximum(best, jnp.abs(pool_v[row_of(layer * cap + c)]))
        top = jnp.max(best.astype(jnp.float32), axis=0, keepdims=True)
        for part in range(SLICES):
            one = top[:, part * half:(part + 1) * half]
            pk_send[layer * SLICES + part] = jnp.concatenate([one] * group, axis=1)
        return carry

    def peak_copy(peer, landing):
        return pltpu.make_async_remote_copy(
            src_ref=pk_send.at[peer], dst_ref=pk_recv.at[landing],
            send_sem=pssem.at[peer], recv_sem=prsem.at[landing],
            device_id={"own": peer}, device_id_type=pl.DeviceIdType.MESH)

    def block_copy(peer, landing):
        return pltpu.make_async_remote_copy(
            src_ref=send.at[peer], dst_ref=recv.at[landing],
            send_sem=ssem.at[peer], recv_sem=rsem.at[landing],
            device_id={"own": peer}, device_id_type=pl.DeviceIdType.MESH)

    def flatten_layer(layer):
        for c in range(cap):
            block = pool_v[row_of(layer * cap + c)].astype(jnp.float32)
            for q in range(tiles):
                lo, hi = q * LANES, min(width, (q + 1) * LANES)
                stage[q, c * tokens:(c + 1) * tokens, 0:hi - lo] = block[:, lo:hi]

        def flatten(i, carry):
            rows_of = [
                jnp.concatenate(
                    [stage[q, pl.ds(i * group + j, cap, stride=tokens), :] for q in range(tiles)], axis=1)
                for j in range(group)
            ]
            for part in range(SLICES):
                joined = jnp.concatenate([r[:, part * half:(part + 1) * half] for r in rows_of], axis=1)
                at = pl.multiple_of(i * period, period)
                send[layer * SLICES + part, :, pl.ds(at, period)] = joined.astype(send.dtype)
            return carry

        lax.fori_loop(0, tokens // group, flatten, 0)

    def start_blocks(layer, parts):
        for part in parts:
            block_copy(layer * SLICES + lax.rem(my_slice + part, SLICES), me).start()

    flattened = set()
    for place, (k, parts) in enumerate(send_order(layers)):
        layer = partner_layer(my_layer, layers, k)
        if k not in flattened:
            flatten_layer(layer)
            flattened.add(k)
        if not place:
            pl.semaphore_wait(barrier, own_n - 1 + rep_n - 1)
        for part in parts:
            block_copy(layer * SLICES + lax.rem(my_slice + part, SLICES), me).start()
        if place == 1:
            lax.fori_loop(0, layers, layer_peak, 0)
            for step in range(1, own_n):
                peak_copy(lax.rem(me + step, own_n), me).start()

    best = pk_send[me]
    for k in range(1, own_n):
        src = lax.rem(me + k, own_n)
        peak_copy(src, src).wait_recv()
        best = jnp.maximum(best, pk_recv[src])
    pk_mine[...] = best

    def rep_copy(mine, table, s_sem, r_sem, peer, landing):
        return pltpu.make_async_remote_copy(
            src_ref=mine, dst_ref=table.at[landing],
            send_sem=s_sem.at[peer], recv_sem=r_sem.at[landing],
            device_id={"rep": peer}, device_id_type=pl.DeviceIdType.MESH)

    for k in range(1, rep_n):
        rep_copy(pk_mine, pk_rep, rpssem, rprsem, lax.rem(rep + k, rep_n), rep).start()
    for k in range(1, rep_n):
        src = lax.rem(rep + k, rep_n)
        rep_copy(pk_mine, pk_rep, rpssem, rprsem, src, src).wait_recv()
        best = jnp.maximum(best, pk_rep[src])

    step = headroom * jnp.maximum(best, 1.0) / 127.0
    inverse = 1.0 / step
    steps_ref[...] = step[:, :half]
    step_wide = jnp.broadcast_to(step, (cap, period))
    inv_wide = jnp.broadcast_to(inverse, (cap, period))

    def encode(source, src, total):
        def one(i, total):
            at = pl.multiple_of(i * period, period)
            x = source[src, :, pl.ds(at, period)].astype(jnp.float32)
            y = jnp.clip(x * inv_wide, -127.0, 127.0).astype(codes_ref.dtype)
            codes_ref[0, 0, src, :, pl.ds(at, period)] = y
            diff = x - y.astype(jnp.float32) * step_wide
            return total + diff * diff
        return lax.fori_loop(0, tokens // group, one, total)

    total = encode(send, me, jnp.zeros((cap, period), jnp.float32))
    for part in range(1, SLICES):
        src = my_layer * SLICES + lax.rem(my_slice + part, SLICES)
        block_copy(src, src).wait_recv()
        total = encode(recv, src, total)
    for k in list(range(layers // 2, layers - 1)) + list(range(layers // 2)):
        layer = partner_layer(my_layer, layers, k)
        for part in range(SLICES):
            src = layer * SLICES + lax.rem(my_slice + part, SLICES)
            block_copy(src, src).wait_recv()
            total = encode(recv, src, total)

    mine = jnp.sum(total, axis=0, keepdims=True)
    er_mine[...] = mine
    for k in range(1, rep_n):
        rep_copy(er_mine, er_rep, ressem, rersem, lax.rem(rep + k, rep_n), rep).start()
    er_rep[rep] = mine
    for k in range(1, rep_n):
        src = lax.rem(rep + k, rep_n)
        rep_copy(er_mine, er_rep, ressem, rersem, src, src).wait_recv()
    whole = er_rep[0]
    for k in range(1, rep_n):
        whole = whole + er_rep[k]
    folded = whole[:, :half]
    for j in range(1, group):
        folded = folded + whole[:, j * half:(j + 1) * half]
    narrow = step[:, :half]
    err_ref[...] = folded / (narrow * narrow * denominator)

    for k in range(1, own_n):
        peer = lax.rem(me + k, own_n)
        peak_copy(peer, me).wait_send()
        block_copy(peer, me).wait_send()
    for k in range(1, rep_n):
        peer = lax.rem(rep + k, rep_n)
        rep_copy(pk_mine, pk_rep, rpssem, rprsem, peer, rep).wait_send()
        rep_copy(er_mine, er_rep, ressem, rersem, peer, rep).wait_send()


def write_out(codes_v, steps_v, err_v, codes_ref, steps_ref, err_ref, sems):
    own_n = codes_v.shape[2]
    moves = [pltpu.make_async_copy(codes_v.at[0, 0, src], codes_ref.at[0, 0, src], sems.at[src])
             for src in range(own_n)]
    moves.append(pltpu.make_async_copy(steps_v, steps_ref, sems.at[own_n]))
    moves.append(pltpu.make_async_copy(err_v, err_ref, sems.at[own_n + 1]))
    for move in moves:
        move.start()
    for move in moves:
        move.wait()


def body(block_pool, sel_index, sel_layer, counts):
    own_n = lax.axis_size("own")
    rep_n = lax.axis_size("rep")
    cap = sel_index.shape[0] // 4
    rows, tokens, width = block_pool.shape
    half = width // SLICES
    flat = tokens * half
    group = LANES // math.gcd(half, LANES)
    period = group * half
    layers = own_n // SLICES
    f32 = jnp.float32
    dma = pltpu.SemaphoreType.DMA
    dtype = block_pool.dtype
    codes, steps, err = pl.pallas_call(
        functools.partial(kernel, own_n, rep_n, cap),
        out_shape=(
            pltpu.VMEM((1, 1, own_n, cap, flat), dtype),
            pltpu.VMEM((1, half), f32),
            pltpu.VMEM((1, half), f32),
        ),
        in_specs=[
            pl.BlockSpec(memory_space=pltpu.SMEM), pl.BlockSpec(memory_space=pltpu.VMEM),
            pl.BlockSpec(memory_space=pltpu.VMEM), pl.BlockSpec(memory_space=pltpu.HBM)],
        out_specs=(
            pl.BlockSpec(memory_space=pltpu.VMEM),
            pl.BlockSpec(memory_space=pltpu.VMEM),
            pl.BlockSpec(memory_space=pltpu.VMEM),
        ),
        scratch_shapes=[
            pltpu.VMEM((layers * cap, LANES), jnp.int32),
            pltpu.SMEM((layers * cap, LANES), jnp.int32),
            pltpu.VMEM((rows + 1, tokens, width), dtype),
            pltpu.VMEM((pl.cdiv(width, LANES), cap * tokens, LANES), f32),
            pltpu.VMEM((own_n, cap, flat), dtype),
            pltpu.VMEM((own_n, cap, flat), dtype),
            pltpu.VMEM((own_n, 1, period), f32),
            pltpu.VMEM((own_n, 1, period), f32),
            pltpu.VMEM((1, period), f32),
            pltpu.VMEM((rep_n, 1, period), f32),
            pltpu.VMEM((1, period), f32),
            pltpu.VMEM((rep_n, 1, period), f32),
            dma, dma((8,)),
            dma((own_n,)), dma((own_n,)), dma((own_n,)), dma((own_n,)),
            dma((rep_n,)), dma((rep_n,)), dma((rep_n,)), dma((rep_n,)),
        ],
        compiler_params=pltpu.CompilerParams(
            collective_id=0, has_side_effects=True, vmem_limit_bytes=(63 * 1024 * 1024 - own_n * cap * flat * 2)),
        name="latent_code",
    )(counts, sel_index[None], sel_layer[None], block_pool)
    hbm = pl.BlockSpec(memory_space=pltpu.HBM)
    return pl.pallas_call(
        write_out,
        out_shape=tuple(jax.ShapeDtypeStruct(x.shape, x.dtype) for x in (codes, steps, err)),
        in_specs=[pl.BlockSpec(memory_space=pltpu.VMEM)] * 3,
        out_specs=(hbm, hbm, hbm),
        scratch_shapes=[dma((own_n + 2,))],
        compiler_params=pltpu.CompilerParams(vmem_limit_bytes=4 * 1024 * 1024),
        name="write_out",
    )(codes, steps, err)


def solution(mesh):
    return jax.shard_map(
        body,
        mesh=mesh,
        in_specs=(
            P(("own", "rep"), None, None),
            P(("own", "rep")),
            P(("own", "rep")),
            P(("own", "rep")),
        ),
        out_specs=(P("own", "rep", None, None, None), P("own", None), P("own", None)),
        check_vma=False,
    )
```

profile of v0, /device:TPU:66, one launch (start us, length us, event | category | flops | bytes accessed | tf_op | source)
XLA Modules:
  0.0 211.4 jit_solution(18059296962118672656)
XLA Ops:
  1.3 206.2 %latent_code.1 = (bf16[1,1,32,8,18432]{4,3,2,1,0:T(8,128)(2,1)S(1)}, f32[1,288]{1,0:T(1,128)S(1)}, f32[1,288]{1,0:T(1,128)S(1)}) custom-call(s32[1]{0:T(128)S(6)} %copy.7.live_ref, s32[1,32]{1,0:T(1,128)} %bitcast.2, s32[1,32]{1,0:T(1,128)} %bitcast.3, bf16[64,64,576]{2,1,0:T(8,128)(2,1)} %pool_ref.1), custom_call_target="tpu_custom_call" | custom-call | tf_op jit(solution)/shard_map/latent_code/pallas_call | solution.py:258
  207.5 3.9 %write_out.1 = (bf16[1,1,32,8,18432]{4,3,2,1,0:T(8,128)(2,1)}, f32[1,288]{1,0:T(1,128)}, f32[1,288]{1,0:T(1,128)}) custom-call(bf16[1,1,32,8,18432]{4,3,2,1,0:T(8,128)(2,1)S(1)} %get-tuple-element.6.codes_v, f32[1,288]{1,0:T(1,128)S(1)} %get-tuple-element.7.steps_v, f32[1,288]{1,0:T(1,128)S(1)} %get-tuple-element.8.err_v), custom_call_target="tpu_custom_call" | custom-call | tf_op jit(solution)/shard_map/write_out/pallas_call | solution.py:295
where the time goes:
time: 212 us; the launch traced here: 211 us
  Pallas kernels  210 us (99%)
    pallas_call x1, Pallas kernels, body(): pl.pallas_call(functools.partial(kernel, own_n, rep_n, cap), out_shape=(p...  206 us

commit v1 on v0

--- a/solution.py
+++ b/solution.py
@@ -13,19 +13,18 @@
 headroom = 0.5
 
 
-def partner_layer(my_layer, layers, k):
-    near = layers // 2
-    if k < near:
-        return lax.rem(my_layer + k, near) + (1 - my_layer // near) * near
-    return lax.rem(my_layer + 1 + k - near, near) + (my_layer // near) * near
-
-
-def send_order(layers):
-    straight, across, both = range(1), range(1, SLICES), range(SLICES)
-    own = [(layers - 1, across)]
-    near = [(k, both) for k in range(layers // 2, layers - 1)]
-    far = [(k, part) for k in range(1, layers // 2) for part in (across, straight)]
-    return [(0, across), (0, straight)] + near + far + own
+SIDE = 4
+ROUNDS = (
+    ((2, 2),), ((2, 0), (0, 2)), ((2, 1), (0, -1)), ((2, -1), (0, 1)),
+    ((1, 2), (-1, 0)), ((-1, 2), (1, 0)), ((1, 1), (-1, -1)), ((1, -1), (-1, 1)),
+)
+
+
+def shifted_layer(my_layer, offset, sign=1):
+    dx, dz = offset
+    x = lax.rem(my_layer // SIDE + sign * dx + SIDE, SIDE)
+    z = lax.rem(my_layer % SIDE + sign * dz + SIDE, SIDE)
+    return x * SIDE + z
 
 
 def fill_slots(live, index_row, layer_row, table, layers, cap, empty):
@@ -136,24 +135,43 @@
 
         lax.fori_loop(0, tokens // group, flatten, 0)
 
-    def start_blocks(layer, parts):
+    def peer_of(offset, part, sign=1):
+        return shifted_layer(my_layer, offset, sign) * SLICES + lax.rem(my_slice + part, SLICES)
+
+    def flatten_to(*offsets):
+        for offset in offsets:
+            flatten_layer(shifted_layer(my_layer, offset))
+
+    def send_to(*offsets):
+        for part in range(SLICES):
+            for offset in offsets:
+                if offset != (0, 0) or part:
+                    block_copy(peer_of(offset, part), me).start()
+
+    sent = set()
+
+    def sent_to(offset, parts=range(SLICES)):
         for part in parts:
-            block_copy(layer * SLICES + lax.rem(my_slice + part, SLICES), me).start()
-
-    flattened = set()
-    for place, (k, parts) in enumerate(send_order(layers)):
-        layer = partner_layer(my_layer, layers, k)
-        if k not in flattened:
-            flatten_layer(layer)
-            flattened.add(k)
-        if not place:
-            pl.semaphore_wait(barrier, own_n - 1 + rep_n - 1)
-        for part in parts:
-            block_copy(layer * SLICES + lax.rem(my_slice + part, SLICES), me).start()
-        if place == 1:
-            lax.fori_loop(0, layers, layer_peak, 0)
-            for step in range(1, own_n):
-                peak_copy(lax.rem(me + step, own_n), me).start()
+            block_copy(peer_of(offset, part), me).wait_send()
+            sent.add((offset, part))
+
+    flatten_to((2, 2))
+    pl.semaphore_wait(barrier, own_n - 1 + rep_n - 1)
+    send_to((2, 2))
+    lax.fori_loop(0, layers, layer_peak, 0)
+    for step in range(1, own_n):
+        peak_copy(lax.rem(me + step, own_n), me).start()
+    for offset in ((2, 0), (2, 1), (2, -1), (0, 0)):
+        flatten_to(offset)
+        send_to(offset)
+    flatten_to((0, 2))
+    sent_to((2, 2))
+    send_to((0, 2))
+    flatten_to((0, -1), (0, 1))
+    for around in ROUNDS[4:]:
+        flatten_to(*around)
+    sent_to((2, 0))
+    send_to((0, -1))
 
     best = pk_send[me]
     for k in range(1, own_n):
@@ -191,17 +209,28 @@
             return total + diff * diff
         return lax.fori_loop(0, tokens // group, one, total)
 
-    total = encode(send, me, jnp.zeros((cap, period), jnp.float32))
-    for part in range(1, SLICES):
-        src = my_layer * SLICES + lax.rem(my_slice + part, SLICES)
-        block_copy(src, src).wait_recv()
-        total = encode(recv, src, total)
-    for k in list(range(layers // 2, layers - 1)) + list(range(layers // 2)):
-        layer = partner_layer(my_layer, layers, k)
+    def take(offset, total):
         for part in range(SLICES):
-            src = layer * SLICES + lax.rem(my_slice + part, SLICES)
+            src = peer_of(offset, part, -1)
             block_copy(src, src).wait_recv()
             total = encode(recv, src, total)
+        return total
+
+    total = encode(send, me, jnp.zeros((cap, period), jnp.float32))
+    src = peer_of((0, 0), 1)
+    block_copy(src, src).wait_recv()
+    total = encode(recv, src, total)
+    total = take((2, 2), total)
+    sent_to((2, 1))
+    send_to((0, 1))
+    total = take((2, 0), total)
+    total = take((0, 2), total)
+    sent_to((2, -1), (0,))
+    for around in ROUNDS[4:]:
+        send_to(*around)
+    for around in ROUNDS[2:]:
+        for offset in around:
+            total = take(offset, total)
 
     mine = jnp.sum(total, axis=0, keepdims=True)
     er_mine[...] = mine
@@ -221,9 +250,11 @@
     err_ref[...] = folded / (narrow * narrow * denominator)
 
     for k in range(1, own_n):
-        peer = lax.rem(me + k, own_n)
-        peak_copy(peer, me).wait_send()
-        block_copy(peer, me).wait_send()
+        peak_copy(lax.rem(me + k, own_n), me).wait_send()
+    for offset in ((0, 0),) + sum(ROUNDS, ()):
+        for part in range(SLICES):
+            if (offset, part) not in sent and (offset, part) != ((0, 0), 0):
+                block_copy(peer_of(offset, part), me).wait_send()
     for k in range(1, rep_n):
         peer = lax.rem(rep + k, rep_n)
         rep_copy(pk_mine, pk_rep, rpssem, rprsem, peer, rep).wait_send()

time: 212 us -> 136 us (0.64)
  the two profiles are of different devices: /device:TPU:66 before, /device:TPU:1 now
where the time goes in v1:
time: 136 us
  Pallas kernels  134 us (99%)
    pallas_call x1, Pallas kernels, body(): pl.pallas_call(functools.partial(kernel, own_n, rep_n, cap), out_shape=(p...  130 us
    pallas_call x1, Pallas kernels, body(): pl.pallas_call(write_out, out_shape=tuple((jax.ShapeDtypeStruct(x.shape,...  3.89 us

profile of v1, /device:TPU:1, one launch (start us, length us, event | category | flops | bytes accessed | tf_op | source)
XLA Modules:
  0.0 135.5 jit_solution(6167755940671122468)
XLA Ops:
  1.3 130.3 %latent_code.1 = (bf16[1,1,32,8,18432]{4,3,2,1,0:T(8,128)(2,1)S(1)}, f32[1,288]{1,0:T(1,128)S(1)}, f32[1,288]{1,0:T(1,128)S(1)}) custom-call(s32[1]{0:T(128)S(6)} %copy.7.live_ref, s32[1,32]{1,0:T(1,128)} %bitcast.2, s32[1,32]{1,0:T(1,128)} %bitcast.3, bf16[64,64,576]{2,1,0:T(8,128)(2,1)} %pool_ref.1), custom_call_target="tpu_custom_call" | custom-call | tf_op jit(solution)/shard_map/latent_code/pallas_call | solution.py:289
  131.6 3.9 %write_out.1 = (bf16[1,1,32,8,18432]{4,3,2,1,0:T(8,128)(2,1)}, f32[1,288]{1,0:T(1,128)}, f32[1,288]{1,0:T(1,128)}) custom-call(bf16[1,1,32,8,18432]{4,3,2,1,0:T(8,128)(2,1)S(1)} %get-tuple-element.6.codes_v, f32[1,288]{1,0:T(1,128)S(1)} %get-tuple-element.7.steps_v, f32[1,288]{1,0:T(1,128)S(1)} %get-tuple-element.8.err_v), custom_call_target="tpu_custom_call" | custom-call | tf_op jit(solution)/shard_map/write_out/pallas_call | solution.py:326

commit v2 on v1

--- a/solution.py
+++ b/solution.py
@@ -27,26 +27,29 @@
     return x * SIDE + z
 
 
-def fill_slots(live, index_row, layer_row, table, layers, cap, empty):
+def fill_slots(live, index_row, layer_row, layers, cap, empty):
     n_select = index_row.shape[1]
-    is_live = lax.broadcasted_iota(jnp.int32, (1, n_select), 1) < live
-    before = lax.broadcasted_iota(jnp.int32, (n_select, n_select), 0)
-    after = lax.broadcasted_iota(jnp.int32, (n_select, n_select), 1)
+    before = lax.broadcasted_iota(jnp.int32, (n_select, n_select), 1)
+    after = lax.broadcasted_iota(jnp.int32, (n_select, n_select), 0)
+    same = before == after
+    layer_col = jnp.sum(jnp.where(same, layer_row, 0), axis=1, keepdims=True)
+    index_col = jnp.sum(jnp.where(same, index_row, 0), axis=1, keepdims=True)
+    is_live = lax.broadcasted_iota(jnp.int32, (n_select, 1), 0) < live
     earlier = jnp.where(before < after, 1.0, 0.0)
-    wanted = lax.broadcasted_iota(jnp.int32, (layers, n_select), 0)
-    matches = jnp.where((layer_row == wanted) & is_live, 1.0, 0.0)
-    ranking = jnp.dot(matches, earlier, preferred_element_type=jnp.float32)
-    slot = lax.broadcasted_iota(jnp.int32, (cap, n_select), 0).astype(jnp.float32)
-    shifted = index_row.astype(jnp.float32) - float(empty)
-    for layer in range(layers):
-        hit = (ranking[layer:layer + 1] == slot) & (matches[layer:layer + 1] > 0.5)
-        found = jnp.sum(jnp.where(hit, shifted, 0.0), axis=1, keepdims=True) + float(empty)
-        table[layer * cap:(layer + 1) * cap, :] = jnp.broadcast_to(found, (cap, LANES)).astype(jnp.int32)
-
-
-def kernel(own_n, rep_n, cap, live_ref, index_ref, layer_ref, pool_ref, codes_ref, steps_ref, err_ref,
-           table, slots, pool_v, stage, send, recv, pk_send, pk_recv, pk_mine, pk_rep, er_mine, er_rep,
-           table_sem, pool_sem, ssem, rsem, pssem, prsem, rpssem, rprsem, ressem, rersem):
+    wanted = lax.broadcasted_iota(jnp.int32, (n_select, LANES), 1)
+    matches = jnp.where((layer_col == wanted) & is_live, 1.0, 0.0)
+    ranking = jnp.dot(earlier, matches, preferred_element_type=jnp.float32)
+    shifted = index_col.astype(jnp.float32) - float(empty)
+    rows = []
+    for slot in range(cap):
+        hit = (ranking == float(slot)) & (matches > 0.5)
+        rows.append(jnp.sum(jnp.where(hit, shifted, 0.0), axis=0, keepdims=True) + float(empty))
+    return jnp.concatenate(rows, axis=0).astype(jnp.int32)
+
+
+def kernel(own_n, rep_n, cap, counts_hbm, index_hbm, layer_hbm, pool_ref, codes_ref, steps_ref, err_ref,
+           live_ref, index_ref, layer_ref, table, slots, pool_v, stage, send, recv, pk_send, pk_recv, pk_mine, pk_rep, er_mine, er_rep,
+           table_sem, small_sem, pool_sem, ssem, rsem, pssem, prsem, rpssem, rprsem, ressem, rersem):
     rows, tokens, width = pool_ref.shape
     half = width // SLICES
     flat = tokens * half
@@ -62,6 +65,10 @@
     pieces = pool_sem.shape[0]
     per_piece = rows // pieces
 
+    small = [
+        pltpu.make_async_copy(src, dst, small_sem.at[i])
+        for i, (src, dst) in enumerate(((counts_hbm, live_ref), (index_hbm, index_ref), (layer_hbm, layer_ref)))
+    ]
     loads = [
         pltpu.make_async_copy(
             pool_ref.at[pl.ds(p * per_piece, per_piece)],
@@ -70,36 +77,45 @@
         )
         for p in range(pieces)
     ]
-    for load in loads:
+
+    def peer_of(offset, part, sign=1):
+        return shifted_layer(my_layer, offset, sign) * SLICES + lax.rem(my_slice + part, SLICES)
+
+    for load in small + loads:
         load.start()
 
     barrier = pltpu.get_barrier_semaphore()
-    for k in range(1, own_n):
-        pl.semaphore_signal(barrier, inc=1, device_id={"own": lax.rem(me + k, own_n)},
+    for offset in sum(ROUNDS, ()):
+        for part in range(SLICES):
+            pl.semaphore_signal(barrier, inc=1, device_id={"own": peer_of(offset, part)},
+                                device_id_type=pl.DeviceIdType.MESH)
+    for part in range(1, SLICES):
+        pl.semaphore_signal(barrier, inc=1, device_id={"own": peer_of((0, 0), part)},
                             device_id_type=pl.DeviceIdType.MESH)
     for k in range(1, rep_n):
         pl.semaphore_signal(barrier, inc=1, device_id={"rep": lax.rem(rep + k, rep_n)},
                             device_id_type=pl.DeviceIdType.MESH)
-
     pool_v[rows] = jnp.zeros((tokens, width), pool_v.dtype)
-    fill_slots(live_ref[0], index_ref[...], layer_ref[...], table, layers, cap, rows)
+    for load in small:
+        load.wait()
+    table[...] = fill_slots(live_ref[0], index_ref[...], layer_ref[...], layers, cap, rows)
     to_scalars = pltpu.make_async_copy(table, slots, table_sem)
     to_scalars.start()
     to_scalars.wait()
     for load in loads:
         load.wait()
 
-    def row_of(slot):
-        return jnp.minimum(jnp.maximum(slots[slot, 0], 0), rows)
+    def row_of(layer, c):
+        return jnp.minimum(jnp.maximum(slots[c, layer], 0), rows)
 
     def layer_peak(layer, carry):
         best = jnp.zeros((tokens, width), pool_v.dtype)
         for c in range(cap):
-            best = jnp.maximum(best, jnp.abs(pool_v[row_of(layer * cap + c)]))
+            best = jnp.maximum(best, jnp.abs(pool_v[row_of(layer, c)]))
         top = jnp.max(best.astype(jnp.float32), axis=0, keepdims=True)
         for part in range(SLICES):
             one = top[:, part * half:(part + 1) * half]
-            pk_send[layer * SLICES + part] = jnp.concatenate([one] * group, axis=1)
+            pk_send[layer * SLICES + part] = one
         return carry
 
     def peak_copy(peer, landing):
@@ -116,7 +132,7 @@
 
     def flatten_layer(layer):
         for c in range(cap):
-            block = pool_v[row_of(layer * cap + c)].astype(jnp.float32)
+            block = pool_v[row_of(layer, c)].astype(jnp.float32)
             for q in range(tiles):
                 lo, hi = q * LANES, min(width, (q + 1) * LANES)
                 stage[q, c * tokens:(c + 1) * tokens, 0:hi - lo] = block[:, lo:hi]
@@ -135,9 +151,6 @@
 
         lax.fori_loop(0, tokens // group, flatten, 0)
 
-    def peer_of(offset, part, sign=1):
-        return shifted_layer(my_layer, offset, sign) * SLICES + lax.rem(my_slice + part, SLICES)
-
     def flatten_to(*offsets):
         for offset in offsets:
             flatten_layer(shifted_layer(my_layer, offset))
@@ -154,6 +167,12 @@
         for part in parts:
             block_copy(peer_of(offset, part), me).wait_send()
             sent.add((offset, part))
+
+    def rep_copy(mine, table, s_sem, r_sem, peer, landing):
+        return pltpu.make_async_remote_copy(
+            src_ref=mine, dst_ref=table.at[landing],
+            send_sem=s_sem.at[peer], recv_sem=r_sem.at[landing],
+            device_id={"rep": peer}, device_id_type=pl.DeviceIdType.MESH)
 
     flatten_to((2, 2))
     pl.semaphore_wait(barrier, own_n - 1 + rep_n - 1)
@@ -167,9 +186,7 @@
     flatten_to((0, 2))
     sent_to((2, 2))
     send_to((0, 2))
-    flatten_to((0, -1), (0, 1))
-    for around in ROUNDS[4:]:
-        flatten_to(*around)
+    flatten_to((0, -1), (0, 1), (1, 2), (-1, 0), (-1, 2), (1, 0))
     sent_to((2, 0))
     send_to((0, -1))
 
@@ -179,23 +196,18 @@
         peak_copy(src, src).wait_recv()
         best = jnp.maximum(best, pk_recv[src])
     pk_mine[...] = best
-
-    def rep_copy(mine, table, s_sem, r_sem, peer, landing):
-        return pltpu.make_async_remote_copy(
-            src_ref=mine, dst_ref=table.at[landing],
-            send_sem=s_sem.at[peer], recv_sem=r_sem.at[landing],
-            device_id={"rep": peer}, device_id_type=pl.DeviceIdType.MESH)
-
     for k in range(1, rep_n):
         rep_copy(pk_mine, pk_rep, rpssem, rprsem, lax.rem(rep + k, rep_n), rep).start()
+    flatten_to((1, 1), (-1, -1), (1, -1), (-1, 1))
     for k in range(1, rep_n):
         src = lax.rem(rep + k, rep_n)
         rep_copy(pk_mine, pk_rep, rpssem, rprsem, src, src).wait_recv()
         best = jnp.maximum(best, pk_rep[src])
 
-    step = headroom * jnp.maximum(best, 1.0) / 127.0
+    narrow = headroom * jnp.maximum(best, 1.0) / 127.0
+    steps_ref[...] = narrow
+    step = jnp.concatenate([narrow] * group, axis=1)
     inverse = 1.0 / step
-    steps_ref[...] = step[:, :half]
     step_wide = jnp.broadcast_to(step, (cap, period))
     inv_wide = jnp.broadcast_to(inverse, (cap, period))
 
@@ -209,28 +221,28 @@
             return total + diff * diff
         return lax.fori_loop(0, tokens // group, one, total)
 
-    def take(offset, total):
-        for part in range(SLICES):
-            src = peer_of(offset, part, -1)
-            block_copy(src, src).wait_recv()
-            total = encode(recv, src, total)
+    def take(total, *offsets):
+        for part in range(SLICES):
+            for offset in offsets:
+                src = peer_of(offset, part, -1)
+                block_copy(src, src).wait_recv()
+                total = encode(recv, src, total)
         return total
 
     total = encode(send, me, jnp.zeros((cap, period), jnp.float32))
     src = peer_of((0, 0), 1)
     block_copy(src, src).wait_recv()
     total = encode(recv, src, total)
-    total = take((2, 2), total)
+    total = take(total, (2, 2))
+    total = take(total, (2, 0))
     sent_to((2, 1))
     send_to((0, 1))
-    total = take((2, 0), total)
-    total = take((0, 2), total)
-    sent_to((2, -1), (0,))
+    total = take(total, (0, 2))
+    sent_to((2, -1))
     for around in ROUNDS[4:]:
         send_to(*around)
     for around in ROUNDS[2:]:
-        for offset in around:
-            total = take(offset, total)
+        total = take(total, *around)
 
     mine = jnp.sum(total, axis=0, keepdims=True)
     er_mine[...] = mine
@@ -246,7 +258,6 @@
     folded = whole[:, :half]
     for j in range(1, group):
         folded = folded + whole[:, j * half:(j + 1) * half]
-    narrow = step[:, :half]
     err_ref[...] = folded / (narrow * narrow * denominator)
 
     for k in range(1, own_n):
@@ -293,28 +304,29 @@
             pltpu.VMEM((1, half), f32),
             pltpu.VMEM((1, half), f32),
         ),
-        in_specs=[
-            pl.BlockSpec(memory_space=pltpu.SMEM), pl.BlockSpec(memory_space=pltpu.VMEM),
-            pl.BlockSpec(memory_space=pltpu.VMEM), pl.BlockSpec(memory_space=pltpu.HBM)],
+        in_specs=[pl.BlockSpec(memory_space=pltpu.HBM)] * 4,
         out_specs=(
             pl.BlockSpec(memory_space=pltpu.VMEM),
             pl.BlockSpec(memory_space=pltpu.VMEM),
             pl.BlockSpec(memory_space=pltpu.VMEM),
         ),
         scratch_shapes=[
-            pltpu.VMEM((layers * cap, LANES), jnp.int32),
-            pltpu.SMEM((layers * cap, LANES), jnp.int32),
+            pltpu.SMEM((1,), jnp.int32),
+            pltpu.VMEM((1, sel_index.shape[0]), jnp.int32),
+            pltpu.VMEM((1, sel_layer.shape[0]), jnp.int32),
+            pltpu.VMEM((cap, LANES), jnp.int32),
+            pltpu.SMEM((cap, LANES), jnp.int32),
             pltpu.VMEM((rows + 1, tokens, width), dtype),
             pltpu.VMEM((pl.cdiv(width, LANES), cap * tokens, LANES), f32),
             pltpu.VMEM((own_n, cap, flat), dtype),
             pltpu.VMEM((own_n, cap, flat), dtype),
-            pltpu.VMEM((own_n, 1, period), f32),
-            pltpu.VMEM((own_n, 1, period), f32),
+            pltpu.VMEM((own_n, 1, half), f32),
+            pltpu.VMEM((own_n, 1, half), f32),
+            pltpu.VMEM((1, half), f32),
+            pltpu.VMEM((rep_n, 1, half), f32),
             pltpu.VMEM((1, period), f32),
             pltpu.VMEM((rep_n, 1, period), f32),
-            pltpu.VMEM((1, period), f32),
-            pltpu.VMEM((rep_n, 1, period), f32),
-            dma, dma((8,)),
+            dma, dma((3,)), dma((8,)),
             dma((own_n,)), dma((own_n,)), dma((own_n,)), dma((own_n,)),
             dma((rep_n,)), dma((rep_n,)), dma((rep_n,)), dma((rep_n,)),
         ],

time: 136 us -> 126 us (0.926)
  Pallas kernels: 134 us -> 124 us
    pallas_call x1, Pallas kernels: 130 us -> 120 us  [body(): pl.pallas_call(functools.partial(kernel, own_n, rep_n, cap), out_shape=(p...]
where the time goes in v2:
time: 126 us
  Pallas kernels  124 us (98%)
  between operations  1.29 us (1%)
    pallas_call x1, Pallas kernels, body(): pl.pallas_call(functools.partial(kernel, own_n, rep_n, cap), out_shape=(p...  120 us
    pallas_call x1, Pallas kernels, body(): pl.pallas_call(write_out, out_shape=tuple((jax.ShapeDtypeStruct(x.shape,...  3.89 us

profile of v2, /device:TPU:1, one launch (start us, length us, event | category | flops | bytes accessed | tf_op | source)
XLA Modules:
  0.0 125.7 jit_solution(8553765041192941044)
XLA Ops:
  1.3 120.5 %latent_code.1 = (bf16[1,1,32,8,18432]{4,3,2,1,0:T(8,128)(2,1)S(1)}, f32[1,288]{1,0:T(1,128)S(1)}, f32[1,288]{1,0:T(1,128)S(1)}) custom-call(s32[1]{0:T(128)S(6)} %copy.7.counts_hbm, s32[1,32]{1,0:T(1,128)} %bitcast.2, s32[1,32]{1,0:T(1,128)} %bitcast.3, bf16[64,64,576]{2,1,0:T(8,128)(2,1)} %pool_ref.1), custom_call_target="tpu_custom_call" | custom-call | tf_op jit(solution)/shard_map/latent_code/pallas_call | solution.py:300
  121.8 3.9 %write_out.1 = (bf16[1,1,32,8,18432]{4,3,2,1,0:T(8,128)(2,1)}, f32[1,288]{1,0:T(1,128)}, f32[1,288]{1,0:T(1,128)}) custom-call(bf16[1,1,32,8,18432]{4,3,2,1,0:T(8,128)(2,1)S(1)} %get-tuple-element.6.codes_v, f32[1,288]{1,0:T(1,128)S(1)} %get-tuple-element.7.steps_v, f32[1,288]{1,0:T(1,128)S(1)} %get-tuple-element.8.err_v), custom_call_target="tpu_custom_call" | custom-call | tf_op jit(solution)/shard_map/write_out/pallas_call | solution.py:338

commit v3 on v2

v3 whole, which is shorter than its diff:
```python
import functools
import math

import jax
import jax.numpy as jnp
from jax import lax
from jax.experimental import pallas as pl
from jax.experimental.pallas import tpu as pltpu
from jax.sharding import PartitionSpec as P

SLICES = 2
LANES = 128
headroom = 0.5


SIDE = 4
ROUNDS = (
    ((2, 2),), ((2, 0), (0, 2)), ((2, 1), (0, -1)), ((2, -1), (0, 1)),
    ((1, 2), (-1, 0)), ((-1, 2), (1, 0)), ((1, 1), (-1, -1)), ((1, -1), (-1, 1)),
)


def shifted_layer(my_layer, offset, sign=1):
    dx, dz = offset
    x = lax.rem(my_layer // SIDE + sign * dx + SIDE, SIDE)
    z = lax.rem(my_layer % SIDE + sign * dz + SIDE, SIDE)
    return x * SIDE + z


def fill_slots(live, index_row, layer_row, layers, cap, empty):
    n_select = index_row.shape[1]
    before = lax.broadcasted_iota(jnp.int32, (n_select, n_select), 1)
    after = lax.broadcasted_iota(jnp.int32, (n_select, n_select), 0)
    same = before == after
    layer_col = jnp.sum(jnp.where(same, layer_row, 0), axis=1, keepdims=True)
    index_col = jnp.sum(jnp.where(same, index_row, 0), axis=1, keepdims=True)
    is_live = lax.broadcasted_iota(jnp.int32, (n_select, 1), 0) < live
    earlier = jnp.where(before < after, 1.0, 0.0)
    wanted = lax.broadcasted_iota(jnp.int32, (n_select, LANES), 1)
    matches = jnp.where((layer_col == wanted) & is_live, 1.0, 0.0)
    ranking = jnp.dot(earlier, matches, preferred_element_type=jnp.float32)
    shifted = index_col.astype(jnp.float32) - float(empty)
    rows = []
    for slot in range(cap):
        hit = (ranking == float(slot)) & (matches > 0.5)
        rows.append(jnp.sum(jnp.where(hit, shifted, 0.0), axis=0, keepdims=True) + float(empty))
    return jnp.concatenate(rows, axis=0).astype(jnp.int32)


def kernel(own_n, rep_n, cap, counts_hbm, index_hbm, layer_hbm, pool_ref, codes_ref, steps_ref, err_ref,
           live_ref, index_ref, layer_ref, table, slots, pool_v, stage, send, recv, pk_send, pk_recv, pk_mine, pk_rep,
           st_mine, st_recv, er_send, er_recv, er_mine, er_rep,
           table_sem, small_sem, pool_sem, ssem, rsem, pssem, prsem, tssem, trsem, essem, ersem,
           rpssem, rprsem, ressem, rersem):
    rows, tokens, width = pool_ref.shape
    half = width // SLICES
    flat = tokens * half
    group = LANES // math.gcd(half, LANES)
    period = group * half
    layers = own_n // SLICES
    me = lax.axis_index("own")
    rep = lax.axis_index("rep")
    my_layer = me // SLICES
    my_slice = me % SLICES
    tiles = stage.shape[0]
    denominator = float(own_n * rep_n * cap * tokens)
    pieces = 8
    per_piece = rows // pieces

    small = [
        pltpu.make_async_copy(src, dst, small_sem.at[i])
        for i, (src, dst) in enumerate(((counts_hbm, live_ref), (index_hbm, index_ref), (layer_hbm, layer_ref)))
    ]
    loads = [
        pltpu.make_async_copy(
            pool_ref.at[pl.ds(p * per_piece, per_piece)],
            pool_v.at[pl.ds(p * per_piece, per_piece)],
            pool_sem,
        )
        for p in range(pieces)
    ]

    def peer_of(offset, part, sign=1):
        return shifted_layer(my_layer, offset, sign) * SLICES + lax.rem(my_slice + part, SLICES)

    for load in small + loads:
        load.start()

    order = [((0, 0), 1)] + [(o, part) for o in sorted(sum(ROUNDS, ()), key=lambda o: o[0] != 0) for part in range(SLICES)]
    single = [(o, part) for around in ROUNDS[4:] for part in range(SLICES) for o in around]
    double = [(0, 0)] + [o for around in ROUNDS[:4] for o in around]

    def place(offset, part):
        return order.index((offset, part))

    def mirrored(offset):
        return tuple(v if v == 2 else -v for v in offset)

    gates = [((2, 2), 0), ((2, 0), 0), ((2, 1), 0), ((2, -1), 0)]

    def sends(offset, part):
        return gates.index((offset, part)) if (offset, part) in gates else len(gates)

    def lands(offset, part):
        return double.index(offset) if offset in double else len(double) + single.index((offset, part))

    barrier = pltpu.get_barrier_semaphore()
    for offset in sum(ROUNDS, ()):
        for part in range(SLICES):
            pl.semaphore_signal(barrier, inc=1, device_id={"own": peer_of(offset, part)},
                                device_id_type=pl.DeviceIdType.MESH)
    for part in range(1, SLICES):
        pl.semaphore_signal(barrier, inc=1, device_id={"own": peer_of((0, 0), part)},
                            device_id_type=pl.DeviceIdType.MESH)
    for k in range(1, rep_n):
        pl.semaphore_signal(barrier, inc=1, device_id={"rep": lax.rem(rep + k, rep_n)},
                            device_id_type=pl.DeviceIdType.MESH)
    pool_v[rows] = jnp.zeros((tokens, width), pool_v.dtype)
    for load in small:
        load.wait()
    table[...] = fill_slots(live_ref[0], index_ref[...], layer_ref[...], layers, cap, rows)
    to_scalars = pltpu.make_async_copy(table, slots, table_sem)
    to_scalars.start()
    to_scalars.wait()
    pltpu.make_async_copy(pool_ref, pool_v.at[pl.ds(0, rows)], pool_sem).wait()

    def row_of(layer, c):
        return jnp.minimum(jnp.maximum(slots[c, layer], 0), rows)

    def layer_peak(layer, carry):
        best = jnp.zeros((tokens, width), pool_v.dtype)
        for c in range(cap):
            best = jnp.maximum(best, jnp.abs(pool_v[row_of(layer, c)]))
        top = jnp.max(best.astype(jnp.float32), axis=0, keepdims=True)
        for part in range(SLICES):
            one = top[:, part * half:(part + 1) * half]
            pk_send[layer * SLICES + part] = one
        return carry

    def over_own(src, dst, s_sem, r_sem, peer):
        return pltpu.make_async_remote_copy(
            src_ref=src, dst_ref=dst, send_sem=s_sem, recv_sem=r_sem,
            device_id={"own": peer}, device_id_type=pl.DeviceIdType.MESH)

    def peak_copy(k):
        peer = lax.rem(me + k, own_n)
        return over_own(pk_send.at[peer], pk_recv.at[k - 1], pssem, prsem, peer)

    def step_copy(offset, part):
        near = 0 if offset[0] == 0 else 1
        return over_own(st_mine, st_recv.at[place(offset, part)], tssem, trsem.at[near], peer_of(offset, part))

    def error_copy(offset, part):
        peer = peer_of(offset, part)
        return over_own(er_send.at[peer], er_recv.at[place(offset, part)], essem, ersem, peer)

    def all_own(src, dst, s_sem, r_sem):
        return over_own(src, dst, s_sem, r_sem, lax.rem(me + 1, own_n))

    def block_copy(offset, part, at=None):
        peer = peer_of(offset, part)
        src, dst = send.at[peer], recv.at[me]
        if at is not None:
            span = pl.ds(at * (flat // 2), flat // 2)
            src, dst = send.at[peer, :, span], recv.at[me, :, span]
        return over_own(src, dst, ssem.at[sends(offset, part)], rsem.at[lands(offset, part)], peer)

    def stage_layer(layer):
        for c in range(cap):
            block = pool_v[row_of(layer, c)].astype(jnp.float32)
            for q in range(tiles):
                lo, hi = q * LANES, min(width, (q + 1) * LANES)
                stage[q, c * tokens:(c + 1) * tokens, 0:hi - lo] = block[:, lo:hi]

    def flatten_part(layer, low, high):
        def flatten(i, carry):
            rows_of = [
                jnp.concatenate(
                    [stage[q, pl.ds(i * group + j, cap, stride=tokens), :] for q in range(tiles)], axis=1)
                for j in range(group)
            ]
            for part in range(SLICES):
                joined = jnp.concatenate([r[:, part * half:(part + 1) * half] for r in rows_of], axis=1)
                at = pl.multiple_of(i * period, period)
                send[layer * SLICES + part, :, pl.ds(at, period)] = joined.astype(send.dtype)
            return carry

        lax.fori_loop(low, high, flatten, 0)

    def flatten_layer(layer):
        stage_layer(layer)
        flatten_part(layer, 0, tokens // group)

    def flatten_to(*offsets):
        for offset in offsets:
            flatten_layer(shifted_layer(my_layer, offset))

    def send_to(*offsets):
        for part in range(SLICES):
            for offset in offsets:
                if offset != (0, 0) or part:
                    block_copy(offset, part).start()

    def released(gate):
        all_own(send.at[0], send.at[0], ssem.at[gate], rsem.at[0]).wait_send()

    def over_rep(src, dst, s_sem, r_sem, k):
        return pltpu.make_async_remote_copy(
            src_ref=src, dst_ref=dst, send_sem=s_sem, recv_sem=r_sem,
            device_id={"rep": lax.rem(rep + k, rep_n)}, device_id_type=pl.DeviceIdType.MESH)

    def rep_copy(mine, table, s_sem, r_sem, k):
        return over_rep(mine, table.at[k - 1], s_sem, r_sem, k)

    def wide(row):
        return jnp.broadcast_to(jnp.concatenate([row] * group, axis=1), (cap, period))

    first = shifted_layer(my_layer, (2, 2))
    stage_layer(first)
    flatten_part(first, 0, tokens // group // 2)
    pl.semaphore_wait(barrier, own_n - 1 + rep_n - 1)
    for part in range(SLICES):
        block_copy((2, 2), part, 0).start()
    flatten_part(first, tokens // group // 2, tokens // group)
    for part in range(SLICES):
        block_copy((2, 2), part, 1).start()
    lax.fori_loop(0, layers, layer_peak, 0)
    for k in range(1, own_n):
        peak_copy(k).start()
    for offset in ((2, 0), (2, 1)):
        flatten_to(offset)
        send_to(offset)
    flatten_to((0, 0), (0, 2), (0, -1))
    send_to((0, 0))
    released(0)
    send_to((0, 2))
    flatten_to((0, 1), (2, -1))

    all_own(pk_recv, pk_recv, pssem, prsem).wait_recv()
    best = jnp.maximum(pk_send[me], jnp.max(pk_recv[...], axis=0))
    pk_mine[...] = best
    for k in range(1, rep_n):
        rep_copy(pk_mine, pk_rep, rpssem, rprsem, k).start()
    flatten_to((1, 2), (-1, 0), (-1, 2))
    over_rep(pk_rep, pk_rep, rpssem, rprsem, 1).wait_recv()
    best = jnp.maximum(best, jnp.max(pk_rep[...], axis=0))

    narrow = headroom * jnp.maximum(best, 1.0) / 127.0
    steps_ref[...] = narrow
    st_mine[...] = narrow
    for offset, part in order:
        step_copy(offset, part).start()
    send_to((2, -1))
    inv_wide = wide(1.0 / narrow)
    released(1)
    send_to((0, -1))
    flatten_to((1, 0), (1, 1), (-1, -1), (1, -1), (-1, 1))

    def encode(source, src):
        def one(i, carry):
            at = pl.multiple_of(i * period, period)
            x = source[src, :, pl.ds(at, period)].astype(jnp.float32)
            codes_ref[0, 0, src, :, pl.ds(at, period)] = jnp.clip(x * inv_wide, -127.0, 127.0).astype(codes_ref.dtype)
            return carry
        lax.fori_loop(0, tokens // group, one, 0)

    def landed(offset, part):
        here = recv.at[pl.ds(0, SLICES if offset in double and offset != (0, 0) else 1)]
        all_own(here, here, ssem.at[0], rsem.at[lands(offset, part)]).wait_recv()

    def take(*offsets, parts=range(SLICES)):
        for part in parts:
            for offset in offsets:
                if offset not in double or not part:
                    landed(offset, part)
                encode(recv, peer_of(offset, part, -1))

    def errors(peer, row):
        step_wide, inverse = wide(row), wide(1.0 / row)

        def one(i, total):
            at = pl.multiple_of(i * period, period)
            x = send[peer, :, pl.ds(at, period)].astype(jnp.float32)
            y = jnp.clip(x * inverse, -127.0, 127.0).astype(codes_ref.dtype)
            diff = x - y.astype(jnp.float32) * step_wide
            return total + diff * diff

        total = lax.fori_loop(0, tokens // group, one, jnp.zeros((cap, period), jnp.float32))
        folded = jnp.sum(total, axis=0, keepdims=True)
        return sum(folded[:, j * half:(j + 1) * half] for j in range(1, group)) + folded[:, :half]

    def errors_to(*offsets):
        for offset in offsets:
            for part in range(SLICES):
                if offset != (0, 0) or part:
                    peer = peer_of(offset, part)
                    er_send[peer] = errors(peer, st_recv[place(mirrored(offset), part)])
                    error_copy(offset, part).start()

    def stepped(near):
        first, count = ((0, n_near), (n_near, len(order) - n_near))[near]
        here = st_recv.at[pl.ds(first, count)]
        all_own(here, here, tssem, trsem.at[near]).wait_recv()

    n_near = sum(offset[0] == 0 for offset, _ in order)
    encode(send, me)
    landed((0, 0), 1)
    encode(recv, peer_of((0, 0), 1))
    take((2, 2))
    released(2)
    send_to((0, 1))
    mine = errors(me, narrow)
    stepped(0)
    errors_to((0, 0), (0, 2), (0, 1), (0, -1))
    take((2, 0))
    take((0, 2))
    released(3)
    for around in ROUNDS[4:6]:
        send_to(*around)
    stepped(1)
    errors_to((1, 0), (-1, 0), (2, 0), (1, 1), (-1, -1), (1, -1), (-1, 1), (2, 1), (2, -1), (1, 2), (-1, 2), (2, 2))
    for around in ROUNDS[6:]:
        send_to(*around)
    for around in ROUNDS[2:7]:
        take(*around)
    all_own(er_recv, er_recv, essem, ersem).wait_recv()
    mine = mine + jnp.sum(er_recv[...], axis=0)
    er_mine[...] = mine
    for k in range(1, rep_n):
        rep_copy(er_mine, er_rep, ressem, rersem, k).start()
    take(*ROUNDS[7], parts=(0,))
    over_rep(er_rep.at[pl.ds(0, rep_n - 1)], er_rep.at[pl.ds(0, rep_n - 1)], ressem, rersem, 1).wait_recv()
    er_rep[rep_n - 1] = mine
    whole = er_rep[lax.rem(rep + rep_n - 1, rep_n)]
    for r in range(1, rep_n):
        whole = whole + er_rep[lax.rem(rep + 2 * rep_n - 1 - r, rep_n)]
    err_ref[...] = whole / (narrow * narrow * denominator)
    others = own_n - 1
    all_own(pk_send.at[pl.ds(0, others)], pk_recv, pssem, prsem).wait_send()
    all_own(st_recv, st_recv, tssem, trsem.at[0]).wait_send()
    all_own(er_send.at[pl.ds(0, others)], er_recv, essem, ersem).wait_send()
    over_rep(pk_rep, pk_rep, rpssem, rprsem, 1).wait_send()
    over_rep(er_rep.at[pl.ds(0, rep_n - 1)], pk_rep, ressem, rersem, 1).wait_send()
    take(*ROUNDS[7], parts=(1,))
    rest = send.at[pl.ds(0, others - len(gates))]
    all_own(rest, rest, ssem.at[len(gates)], rsem.at[0]).wait_send()


def write_out(codes_v, steps_v, err_v, codes_ref, steps_ref, err_ref, sems):
    own_n = codes_v.shape[2]
    pieces = 8
    per_piece = own_n // pieces
    for p in range(pieces):
        at = pl.ds(p * per_piece, per_piece)
        pltpu.make_async_copy(codes_v.at[:, :, at], codes_ref.at[:, :, at], sems.at[0]).start()
    moves = [pltpu.make_async_copy(steps_v, steps_ref, sems.at[1]), pltpu.make_async_copy(err_v, err_ref, sems.at[2])]
    for move in moves:
        move.start()
    for move in moves:
        move.wait()
    pltpu.make_async_copy(codes_v, codes_ref, sems.at[0]).wait()


def body(block_pool, sel_index, sel_layer, counts):
    own_n = lax.axis_size("own")
    rep_n = lax.axis_size("rep")
    cap = sel_index.shape[0] // 4
    rows, tokens, width = block_pool.shape
    half = width // SLICES
    flat = tokens * half
    group = LANES // math.gcd(half, LANES)
    period = group * half
    layers = own_n // SLICES
    f32 = jnp.float32
    dma = pltpu.SemaphoreType.DMA
    dtype = block_pool.dtype
    codes, steps, err = pl.pallas_call(
        functools.partial(kernel, own_n, rep_n, cap),
        out_shape=(
            pltpu.VMEM((1, 1, own_n, cap, flat), dtype),
            pltpu.VMEM((1, half), f32),
            pltpu.VMEM((1, half), f32),
        ),
        in_specs=[pl.BlockSpec(memory_space=pltpu.HBM)] * 4,
        out_specs=(
            pl.BlockSpec(memory_space=pltpu.VMEM),
            pl.BlockSpec(memory_space=pltpu.VMEM),
            pl.BlockSpec(memory_space=pltpu.VMEM),
        ),
        scratch_shapes=[
            pltpu.SMEM((1,), jnp.int32),
            pltpu.VMEM((1, sel_index.shape[0]), jnp.int32),
            pltpu.VMEM((1, sel_layer.shape[0]), jnp.int32),
            pltpu.VMEM((cap, LANES), jnp.int32),
            pltpu.SMEM((cap, LANES), jnp.int32),
            pltpu.VMEM((rows + 1, tokens, width), dtype),
            pltpu.VMEM((pl.cdiv(width, LANES), cap * tokens, LANES), f32),
            pltpu.VMEM((own_n, cap, flat), dtype),
            pltpu.VMEM((own_n, cap, flat), dtype),
            pltpu.VMEM((own_n, 1, half), f32),
            pltpu.VMEM((own_n - 1, 1, half), f32),
            pltpu.VMEM((1, half), f32),
            pltpu.VMEM((rep_n - 1, 1, half), f32),
            pltpu.VMEM((1, half), f32),
            pltpu.VMEM((own_n - 1, 1, half), f32),
            pltpu.VMEM((own_n, 1, half), f32),
            pltpu.VMEM((own_n - 1, 1, half), f32),
            pltpu.VMEM((1, half), f32),
            pltpu.VMEM((rep_n, 1, half), f32),
            dma, dma((3,)), dma,
            dma((5,)), dma((24,)), dma, dma, dma, dma((2,)), dma, dma,
            dma, dma, dma, dma,
        ],
        compiler_params=pltpu.CompilerParams(
            collective_id=0, has_side_effects=True, vmem_limit_bytes=(63 * 1024 * 1024 - own_n * cap * flat * 2)),
        name="latent_code",
    )(counts, sel_index[None], sel_layer[None], block_pool)
    hbm = pl.BlockSpec(memory_space=pltpu.HBM)
    return pl.pallas_call(
        write_out,
        out_shape=tuple(jax.ShapeDtypeStruct(x.shape, x.dtype) for x in (codes, steps, err)),
        in_specs=[pl.BlockSpec(memory_space=pltpu.VMEM)] * 3,
        out_specs=(hbm, hbm, hbm),
        scratch_shapes=[dma((3,))],
        compiler_params=pltpu.CompilerParams(vmem_limit_bytes=4 * 1024 * 1024),
        name="write_out",
    )(codes, steps, err)


def solution(mesh):
    return jax.shard_map(
        body,
        mesh=mesh,
        in_specs=(
            P(("own", "rep"), None, None),
            P(("own", "rep")),
            P(("own", "rep")),
            P(("own", "rep")),
        ),
        out_specs=(P("own", "rep", None, None, None), P("own", None), P("own", None)),
        check_vma=False,
    )
```

time: 126 us -> 121 us (0.960)
  Pallas kernels: 124 us -> 119 us
    pallas_call x1, Pallas kernels: 120 us -> 115 us  [body(): pl.pallas_call(functools.partial(kernel, own_n, rep_n, cap), out_shape=(p...]
where the time goes in v3:
time: 121 us; the launch traced here: 120 us
  Pallas kernels  119 us (98%)
  between operations  1.29 us (1%)
    pallas_call x1, Pallas kernels, body(): pl.pallas_call(functools.partial(kernel, own_n, rep_n, cap), out_shape=(p...  115 us
    pallas_call x1, Pallas kernels, body(): pl.pallas_call(write_out, out_shape=tuple((jax.ShapeDtypeStruct(x.shape,...  3.66 us

profile of v3, /device:TPU:1, one launch (start us, length us, event | category | flops | bytes accessed | tf_op | source)
XLA Modules:
  0.0 120.4 jit_solution(4658676715977848282)
XLA Ops:
  1.3 115.5 %latent_code.1 = (bf16[1,1,32,8,18432]{4,3,2,1,0:T(8,128)(2,1)S(1)}, f32[1,288]{1,0:T(1,128)S(1)}, f32[1,288]{1,0:T(1,128)S(1)}) custom-call(s32[1]{0:T(128)S(6)} %copy.7.counts_hbm, s32[1,32]{1,0:T(1,128)} %bitcast.2, s32[1,32]{1,0:T(1,128)} %bitcast.3, bf16[64,64,576]{2,1,0:T(8,128)(2,1)} %pool_ref.1), custom_call_target="tpu_custom_call" | custom-call | tf_op jit(solution)/shard_map/latent_code/pallas_call | solution.py:377
  116.7 3.7 %write_out.1 = (bf16[1,1,32,8,18432]{4,3,2,1,0:T(8,128)(2,1)}, f32[1,288]{1,0:T(1,128)}, f32[1,288]{1,0:T(1,128)}) custom-call(bf16[1,1,32,8,18432]{4,3,2,1,0:T(8,128)(2,1)S(1)} %get-tuple-element.6.codes_v, f32[1,288]{1,0:T(1,128)S(1)} %get-tuple-element.7.steps_v, f32[1,288]{1,0:T(1,128)S(1)} %get-tuple-element.8.err_v), custom_call_target="tpu_custom_call" | custom-call | tf_op jit(solution)/shard_map/write_out/pallas_call | solution.py:419

commit v4 on v3

--- a/solution.py
+++ b/solution.py
@@ -10,6 +10,7 @@
 
 SLICES = 2
 LANES = 128
+PIECES = 4
 headroom = 0.5
 
 
@@ -47,8 +48,8 @@
     return jnp.concatenate(rows, axis=0).astype(jnp.int32)
 
 
-def kernel(own_n, rep_n, cap, counts_hbm, index_hbm, layer_hbm, pool_ref, codes_ref, steps_ref, err_ref,
-           live_ref, index_ref, layer_ref, table, slots, pool_v, stage, send, recv, pk_send, pk_recv, pk_mine, pk_rep,
+def kernel(own_n, rep_n, cap, live_ref, index_hbm, layer_hbm, pool_ref, codes_ref, steps_ref, err_ref,
+           index_ref, layer_ref, table, slots, pool_v, stage, send, recv, pk_send, pk_recv, pk_mine, pk_rep,
            st_mine, st_recv, er_send, er_recv, er_mine, er_rep,
            table_sem, small_sem, pool_sem, ssem, rsem, pssem, prsem, tssem, trsem, essem, ersem,
            rpssem, rprsem, ressem, rersem):
@@ -69,7 +70,7 @@
 
     small = [
         pltpu.make_async_copy(src, dst, small_sem.at[i])
-        for i, (src, dst) in enumerate(((counts_hbm, live_ref), (index_hbm, index_ref), (layer_hbm, layer_ref)))
+        for i, (src, dst) in enumerate(((index_hbm, index_ref), (layer_hbm, layer_ref)))
     ]
     loads = [
         pltpu.make_async_copy(
@@ -83,10 +84,10 @@
     def peer_of(offset, part, sign=1):
         return shifted_layer(my_layer, offset, sign) * SLICES + lax.rem(my_slice + part, SLICES)
 
-    for load in small + loads:
+    for load in small:
         load.start()
 
-    order = [((0, 0), 1)] + [(o, part) for o in sorted(sum(ROUNDS, ()), key=lambda o: o[0] != 0) for part in range(SLICES)]
+    order = [(o, part) for o in sum(ROUNDS, ()) if o[0] for part in range(SLICES)]
     single = [(o, part) for around in ROUNDS[4:] for part in range(SLICES) for o in around]
     double = [(0, 0)] + [o for around in ROUNDS[:4] for o in around]
 
@@ -115,6 +116,8 @@
     for k in range(1, rep_n):
         pl.semaphore_signal(barrier, inc=1, device_id={"rep": lax.rem(rep + k, rep_n)},
                             device_id_type=pl.DeviceIdType.MESH)
+    for load in loads:
+        load.start()
     pool_v[rows] = jnp.zeros((tokens, width), pool_v.dtype)
     for load in small:
         load.wait()
@@ -147,8 +150,7 @@
         return over_own(pk_send.at[peer], pk_recv.at[k - 1], pssem, prsem, peer)
 
     def step_copy(offset, part):
-        near = 0 if offset[0] == 0 else 1
-        return over_own(st_mine, st_recv.at[place(offset, part)], tssem, trsem.at[near], peer_of(offset, part))
+        return over_own(st_mine, st_recv.at[place(offset, part)], tssem, trsem, peer_of(offset, part))
 
     def error_copy(offset, part):
         peer = peer_of(offset, part)
@@ -161,7 +163,7 @@
         peer = peer_of(offset, part)
         src, dst = send.at[peer], recv.at[me]
         if at is not None:
-            span = pl.ds(at * (flat // 2), flat // 2)
+            span = pl.ds(at * (flat // PIECES), flat // PIECES)
             src, dst = send.at[peer, :, span], recv.at[me, :, span]
         return over_own(src, dst, ssem.at[sends(offset, part)], rsem.at[lands(offset, part)], peer)
 
@@ -217,13 +219,12 @@
 
     first = shifted_layer(my_layer, (2, 2))
     stage_layer(first)
-    flatten_part(first, 0, tokens // group // 2)
-    pl.semaphore_wait(barrier, own_n - 1 + rep_n - 1)
-    for part in range(SLICES):
-        block_copy((2, 2), part, 0).start()
-    flatten_part(first, tokens // group // 2, tokens // group)
-    for part in range(SLICES):
-        block_copy((2, 2), part, 1).start()
+    for at in range(PIECES):
+        flatten_part(first, at * (tokens // group // PIECES), (at + 1) * (tokens // group // PIECES))
+        if not at:
+            pl.semaphore_wait(barrier, own_n - 1 + rep_n - 1)
+        for part in range(SLICES):
+            block_copy((2, 2), part, at).start()
     lax.fori_loop(0, layers, layer_peak, 0)
     for k in range(1, own_n):
         peak_copy(k).start()
@@ -251,7 +252,7 @@
     for offset, part in order:
         step_copy(offset, part).start()
     send_to((2, -1))
-    inv_wide = wide(1.0 / narrow)
+    inv_wide, step_wide = wide(1.0 / narrow), wide(narrow)
     released(1)
     send_to((0, -1))
     flatten_to((1, 0), (1, 1), (-1, -1), (1, -1), (-1, 1))
@@ -264,6 +265,20 @@
             return carry
         lax.fori_loop(0, tokens // group, one, 0)
 
+    def encode_and_sum(source, src, total):
+        def one(i, total):
+            at = pl.multiple_of(i * period, period)
+            x = source[src, :, pl.ds(at, period)].astype(jnp.float32)
+            y = jnp.clip(x * inv_wide, -127.0, 127.0).astype(codes_ref.dtype)
+            codes_ref[0, 0, src, :, pl.ds(at, period)] = y
+            diff = x - y.astype(jnp.float32) * step_wide
+            return total + diff * diff
+        return lax.fori_loop(0, tokens // group, one, total)
+
+    def fold(total):
+        row = jnp.sum(total, axis=0, keepdims=True)
+        return sum(row[:, j * half:(j + 1) * half] for j in range(1, group)) + row[:, :half]
+
     def landed(offset, part):
         here = recv.at[pl.ds(0, SLICES if offset in double and offset != (0, 0) else 1)]
         all_own(here, here, ssem.at[0], rsem.at[lands(offset, part)]).wait_recv()
@@ -275,54 +290,52 @@
                     landed(offset, part)
                 encode(recv, peer_of(offset, part, -1))
 
+    def take_and_sum(total, *offsets):
+        for offset in offsets:
+            landed(offset, 0)
+            for part in range(SLICES):
+                total = encode_and_sum(recv, peer_of(offset, part, -1), total)
+        return total
+
     def errors(peer, row):
-        step_wide, inverse = wide(row), wide(1.0 / row)
+        peer_step, peer_inverse = wide(row), wide(1.0 / row)
 
         def one(i, total):
             at = pl.multiple_of(i * period, period)
             x = send[peer, :, pl.ds(at, period)].astype(jnp.float32)
-            y = jnp.clip(x * inverse, -127.0, 127.0).astype(codes_ref.dtype)
-            diff = x - y.astype(jnp.float32) * step_wide
+            y = jnp.clip(x * peer_inverse, -127.0, 127.0).astype(codes_ref.dtype)
+            diff = x - y.astype(jnp.float32) * peer_step
             return total + diff * diff
 
-        total = lax.fori_loop(0, tokens // group, one, jnp.zeros((cap, period), jnp.float32))
-        folded = jnp.sum(total, axis=0, keepdims=True)
-        return sum(folded[:, j * half:(j + 1) * half] for j in range(1, group)) + folded[:, :half]
+        return fold(lax.fori_loop(0, tokens // group, one, jnp.zeros((cap, period), jnp.float32)))
 
     def errors_to(*offsets):
         for offset in offsets:
             for part in range(SLICES):
-                if offset != (0, 0) or part:
-                    peer = peer_of(offset, part)
-                    er_send[peer] = errors(peer, st_recv[place(mirrored(offset), part)])
-                    error_copy(offset, part).start()
-
-    def stepped(near):
-        first, count = ((0, n_near), (n_near, len(order) - n_near))[near]
-        here = st_recv.at[pl.ds(first, count)]
-        all_own(here, here, tssem, trsem.at[near]).wait_recv()
-
-    n_near = sum(offset[0] == 0 for offset, _ in order)
-    encode(send, me)
-    landed((0, 0), 1)
-    encode(recv, peer_of((0, 0), 1))
+                peer = peer_of(offset, part)
+                er_send[peer] = errors(peer, st_recv[place(mirrored(offset), part)])
+                error_copy(offset, part).start()
+
     take((2, 2))
     released(2)
     send_to((0, 1))
-    mine = errors(me, narrow)
-    stepped(0)
-    errors_to((0, 0), (0, 2), (0, 1), (0, -1))
+    total = encode_and_sum(send, me, jnp.zeros((cap, period), jnp.float32))
+    landed((0, 0), 1)
+    total = encode_and_sum(recv, peer_of((0, 0), 1), total)
     take((2, 0))
-    take((0, 2))
+    total = take_and_sum(total, (0, 2))
     released(3)
     for around in ROUNDS[4:6]:
         send_to(*around)
-    stepped(1)
+    all_own(st_recv, st_recv, tssem, trsem).wait_recv()
     errors_to((1, 0), (-1, 0), (2, 0), (1, 1), (-1, -1), (1, -1), (-1, 1), (2, 1), (2, -1), (1, 2), (-1, 2), (2, 2))
     for around in ROUNDS[6:]:
         send_to(*around)
-    for around in ROUNDS[2:7]:
+    take((2, 1))
+    take((2, -1))
+    for around in ROUNDS[4:7]:
         take(*around)
+    mine = fold(take_and_sum(total, (0, -1), (0, 1)))
     all_own(er_recv, er_recv, essem, ersem).wait_recv()
     mine = mine + jnp.sum(er_recv[...], axis=0)
     er_mine[...] = mine
@@ -337,8 +350,8 @@
     err_ref[...] = whole / (narrow * narrow * denominator)
     others = own_n - 1
     all_own(pk_send.at[pl.ds(0, others)], pk_recv, pssem, prsem).wait_send()
-    all_own(st_recv, st_recv, tssem, trsem.at[0]).wait_send()
-    all_own(er_send.at[pl.ds(0, others)], er_recv, essem, ersem).wait_send()
+    all_own(st_recv, st_recv, tssem, trsem).wait_send()
+    all_own(er_recv, er_recv, essem, ersem).wait_send()
     over_rep(pk_rep, pk_rep, rpssem, rprsem, 1).wait_send()
     over_rep(er_rep.at[pl.ds(0, rep_n - 1)], pk_rep, ressem, rersem, 1).wait_send()
     take(*ROUNDS[7], parts=(1,))
@@ -381,14 +394,13 @@
             pltpu.VMEM((1, half), f32),
             pltpu.VMEM((1, half), f32),
         ),
-        in_specs=[pl.BlockSpec(memory_space=pltpu.HBM)] * 4,
+        in_specs=[pl.BlockSpec(memory_space=pltpu.SMEM)] + [pl.BlockSpec(memory_space=pltpu.HBM)] * 3,
         out_specs=(
             pl.BlockSpec(memory_space=pltpu.VMEM),
             pl.BlockSpec(memory_space=pltpu.VMEM),
             pl.BlockSpec(memory_space=pltpu.VMEM),
         ),
         scratch_shapes=[
-            pltpu.SMEM((1,), jnp.int32),
             pltpu.VMEM((1, sel_index.shape[0]), jnp.int32),
             pltpu.VMEM((1, sel_layer.shape[0]), jnp.int32),
             pltpu.VMEM((cap, LANES), jnp.int32),
@@ -402,13 +414,13 @@
             pltpu.VMEM((1, half), f32),
             pltpu.VMEM((rep_n - 1, 1, half), f32),
             pltpu.VMEM((1, half), f32),
-            pltpu.VMEM((own_n - 1, 1, half), f32),
+            pltpu.VMEM((own_n - SIDE * SLICES, 1, half), f32),
             pltpu.VMEM((own_n, 1, half), f32),
-            pltpu.VMEM((own_n - 1, 1, half), f32),
+            pltpu.VMEM((own_n - SIDE * SLICES, 1, half), f32),
             pltpu.VMEM((1, half), f32),
             pltpu.VMEM((rep_n, 1, half), f32),
-            dma, dma((3,)), dma,
-            dma((5,)), dma((24,)), dma, dma, dma, dma((2,)), dma, dma,
+            dma, dma((2,)), dma,
+            dma((5,)), dma((24,)), dma, dma, dma, dma, dma, dma,
             dma, dma, dma, dma,
         ],
         compiler_params=pltpu.CompilerParams(

time: 121 us -> 120 us (level)
  no operation moved by 1% of the time
where the time goes in v4:
time: 120 us
  Pallas kernels  119 us (99%)
  between operations  1.29 us (1%)
    pallas_call x1, Pallas kernels, body(): pl.pallas_call(functools.partial(kernel, own_n, rep_n, cap), out_shape=(p...  115 us
    pallas_call x1, Pallas kernels, body(): pl.pallas_call(write_out, out_shape=tuple((jax.ShapeDtypeStruct(x.shape,...  3.66 us

profile of v4, /device:TPU:1, one launch (start us, length us, event | category | flops | bytes accessed | tf_op | source)
XLA Modules:
  0.0 119.9 jit_solution(16107432948730972190)
XLA Ops:
  1.3 115.0 %latent_code.1 = (bf16[1,1,32,8,18432]{4,3,2,1,0:T(8,128)(2,1)S(1)}, f32[1,288]{1,0:T(1,128)S(1)}, f32[1,288]{1,0:T(1,128)S(1)}) custom-call(s32[1]{0:T(128)S(6)} %copy.7.live_ref, s32[1,32]{1,0:T(1,128)} %bitcast.2, s32[1,32]{1,0:T(1,128)} %bitcast.3, bf16[64,64,576]{2,1,0:T(8,128)(2,1)} %pool_ref.1), custom_call_target="tpu_custom_call" | custom-call | tf_op jit(solution)/shard_map/latent_code/pallas_call | solution.py:390
  116.3 3.7 %write_out.1 = (bf16[1,1,32,8,18432]{4,3,2,1,0:T(8,128)(2,1)}, f32[1,288]{1,0:T(1,128)}, f32[1,288]{1,0:T(1,128)}) custom-call(bf16[1,1,32,8,18432]{4,3,2,1,0:T(8,128)(2,1)S(1)} %get-tuple-element.6.codes_v, f32[1,288]{1,0:T(1,128)S(1)} %get-tuple-element.7.steps_v, f32[1,288]{1,0:T(1,128)S(1)} %get-tuple-element.8.err_v), custom_call_target="tpu_custom_call" | custom-call | tf_op jit(solution)/shard_map/write_out/pallas_call | solution.py:431

commit v5 on v4

--- a/solution.py
+++ b/solution.py
@@ -87,7 +87,7 @@
     for load in small:
         load.start()
 
-    order = [(o, part) for o in sum(ROUNDS, ()) if o[0] for part in range(SLICES)]
+    order = [(o, part) for o in ROUNDS[7] for part in range(SLICES)]
     single = [(o, part) for around in ROUNDS[4:] for part in range(SLICES) for o in around]
     double = [(0, 0)] + [o for around in ROUNDS[:4] for o in around]
 
@@ -137,7 +137,7 @@
         top = jnp.max(best.astype(jnp.float32), axis=0, keepdims=True)
         for part in range(SLICES):
             one = top[:, part * half:(part + 1) * half]
-            pk_send[layer * SLICES + part] = one
+            pk_send[layer * SLICES + part] = one.astype(pk_send.dtype)
         return carry
 
     def over_own(src, dst, s_sem, r_sem, peer):
@@ -153,8 +153,8 @@
         return over_own(st_mine, st_recv.at[place(offset, part)], tssem, trsem, peer_of(offset, part))
 
     def error_copy(offset, part):
-        peer = peer_of(offset, part)
-        return over_own(er_send.at[peer], er_recv.at[place(offset, part)], essem, ersem, peer)
+        at = place(offset, part)
+        return over_own(er_send.at[at], er_recv.at[at], essem, ersem, peer_of(offset, part))
 
     def all_own(src, dst, s_sem, r_sem):
         return over_own(src, dst, s_sem, r_sem, lax.rem(me + 1, own_n))
@@ -238,7 +238,7 @@
     flatten_to((0, 1), (2, -1))
 
     all_own(pk_recv, pk_recv, pssem, prsem).wait_recv()
-    best = jnp.maximum(pk_send[me], jnp.max(pk_recv[...], axis=0))
+    best = jnp.maximum(pk_send[me].astype(jnp.float32), jnp.max(pk_recv[...].astype(jnp.float32), axis=0))
     pk_mine[...] = best
     for k in range(1, rep_n):
         rep_copy(pk_mine, pk_rep, rpssem, rprsem, k).start()
@@ -291,9 +291,10 @@
                 encode(recv, peer_of(offset, part, -1))
 
     def take_and_sum(total, *offsets):
-        for offset in offsets:
-            landed(offset, 0)
-            for part in range(SLICES):
+        for part in range(SLICES):
+            for offset in offsets:
+                if offset not in double or not part:
+                    landed(offset, part)
                 total = encode_and_sum(recv, peer_of(offset, part, -1), total)
         return total
 
@@ -312,29 +313,28 @@
     def errors_to(*offsets):
         for offset in offsets:
             for part in range(SLICES):
-                peer = peer_of(offset, part)
-                er_send[peer] = errors(peer, st_recv[place(mirrored(offset), part)])
+                er_send[place(offset, part)] = errors(peer_of(offset, part), st_recv[place(mirrored(offset), part)])
                 error_copy(offset, part).start()
 
-    take((2, 2))
+    total = encode_and_sum(send, me, jnp.zeros((cap, period), jnp.float32))
     released(2)
     send_to((0, 1))
-    total = encode_and_sum(send, me, jnp.zeros((cap, period), jnp.float32))
     landed((0, 0), 1)
     total = encode_and_sum(recv, peer_of((0, 0), 1), total)
-    take((2, 0))
+    total = take_and_sum(total, (2, 2))
+    total = take_and_sum(total, (2, 0))
     total = take_and_sum(total, (0, 2))
     released(3)
     for around in ROUNDS[4:6]:
         send_to(*around)
     all_own(st_recv, st_recv, tssem, trsem).wait_recv()
-    errors_to((1, 0), (-1, 0), (2, 0), (1, 1), (-1, -1), (1, -1), (-1, 1), (2, 1), (2, -1), (1, 2), (-1, 2), (2, 2))
+    errors_to(*ROUNDS[7])
     for around in ROUNDS[6:]:
         send_to(*around)
-    take((2, 1))
-    take((2, -1))
+    total = take_and_sum(total, (2, 1))
+    total = take_and_sum(total, (2, -1))
     for around in ROUNDS[4:7]:
-        take(*around)
+        total = take_and_sum(total, *around)
     mine = fold(take_and_sum(total, (0, -1), (0, 1)))
     all_own(er_recv, er_recv, essem, ersem).wait_recv()
     mine = mine + jnp.sum(er_recv[...], axis=0)
@@ -409,14 +409,14 @@
             pltpu.VMEM((pl.cdiv(width, LANES), cap * tokens, LANES), f32),
             pltpu.VMEM((own_n, cap, flat), dtype),
             pltpu.VMEM((own_n, cap, flat), dtype),
-            pltpu.VMEM((own_n, 1, half), f32),
-            pltpu.VMEM((own_n - 1, 1, half), f32),
+            pltpu.VMEM((own_n, 1, half), dtype),
+            pltpu.VMEM((own_n - 1, 1, half), dtype),
             pltpu.VMEM((1, half), f32),
             pltpu.VMEM((rep_n - 1, 1, half), f32),
             pltpu.VMEM((1, half), f32),
-            pltpu.VMEM((own_n - SIDE * SLICES, 1, half), f32),
-            pltpu.VMEM((own_n, 1, half), f32),
-            pltpu.VMEM((own_n - SIDE * SLICES, 1, half), f32),
+            pltpu.VMEM((len(ROUNDS[7]) * SLICES, 1, half), f32),
+            pltpu.VMEM((len(ROUNDS[7]) * SLICES, 1, half), f32),
+            pltpu.VMEM((len(ROUNDS[7]) * SLICES, 1, half), f32),
             pltpu.VMEM((1, half), f32),
             pltpu.VMEM((rep_n, 1, half), f32),
             dma, dma((2,)), dma,

time: 120 us -> 119 us (level)
  no operation moved by 1% of the time
where the time goes in v5:
time: 119 us
  Pallas kernels  118 us (99%)
  between operations  1.29 us (1%)
    pallas_call x1, Pallas kernels, body(): pl.pallas_call(functools.partial(kernel, own_n, rep_n, cap), out_shape=(p...  114 us
    pallas_call x1, Pallas kernels, body(): pl.pallas_call(write_out, out_shape=tuple((jax.ShapeDtypeStruct(x.shape,...  3.66 us

profile of v5, /device:TPU:1, one launch (start us, length us, event | category | flops | bytes accessed | tf_op | source)
XLA Modules:
  0.0 119.2 jit_solution(3253583937008799696)
XLA Ops:
  1.3 114.3 %latent_code.1 = (bf16[1,1,32,8,18432]{4,3,2,1,0:T(8,128)(2,1)S(1)}, f32[1,288]{1,0:T(1,128)S(1)}, f32[1,288]{1,0:T(1,128)S(1)}) custom-call(s32[1]{0:T(128)S(6)} %copy.7.live_ref, s32[1,32]{1,0:T(1,128)} %bitcast.2, s32[1,32]{1,0:T(1,128)} %bitcast.3, bf16[64,64,576]{2,1,0:T(8,128)(2,1)} %pool_ref.1), custom_call_target="tpu_custom_call" | custom-call | tf_op jit(solution)/shard_map/latent_code/pallas_call | solution.py:390
  115.5 3.7 %write_out.1 = (bf16[1,1,32,8,18432]{4,3,2,1,0:T(8,128)(2,1)}, f32[1,288]{1,0:T(1,128)}, f32[1,288]{1,0:T(1,128)}) custom-call(bf16[1,1,32,8,18432]{4,3,2,1,0:T(8,128)(2,1)S(1)} %get-tuple-element.6.codes_v, f32[1,288]{1,0:T(1,128)S(1)} %get-tuple-element.7.steps_v, f32[1,288]{1,0:T(1,128)S(1)} %get-tuple-element.8.err_v), custom_call_target="tpu_custom_call" | custom-call | tf_op jit(solution)/shard_map/write_out/pallas_call | solution.py:431

commit v6 on v5

--- a/solution.py
+++ b/solution.py
@@ -10,7 +10,7 @@
 
 SLICES = 2
 LANES = 128
-PIECES = 4
+PIECES = 8
 headroom = 0.5
 
 
@@ -88,8 +88,8 @@
         load.start()
 
     order = [(o, part) for o in ROUNDS[7] for part in range(SLICES)]
-    single = [(o, part) for around in ROUNDS[4:] for part in range(SLICES) for o in around]
-    double = [(0, 0)] + [o for around in ROUNDS[:4] for o in around]
+    single = [(o, part) for around in ROUNDS[7:] for part in range(SLICES) for o in around]
+    double = [(0, 0)] + [o for around in ROUNDS[:7] for o in around]
 
     def place(offset, part):
         return order.index((offset, part))
@@ -317,12 +317,12 @@
                 error_copy(offset, part).start()
 
     total = encode_and_sum(send, me, jnp.zeros((cap, period), jnp.float32))
-    released(2)
-    send_to((0, 1))
     landed((0, 0), 1)
     total = encode_and_sum(recv, peer_of((0, 0), 1), total)
     total = take_and_sum(total, (2, 2))
     total = take_and_sum(total, (2, 0))
+    released(2)
+    send_to((0, 1))
     total = take_and_sum(total, (0, 2))
     released(3)
     for around in ROUNDS[4:6]:
@@ -420,7 +420,7 @@
             pltpu.VMEM((1, half), f32),
             pltpu.VMEM((rep_n, 1, half), f32),
             dma, dma((2,)), dma,
-            dma((5,)), dma((24,)), dma, dma, dma, dma, dma, dma,
+            dma((5,)), dma((18,)), dma, dma, dma, dma, dma, dma,
             dma, dma, dma, dma,
         ],
         compiler_params=pltpu.CompilerParams(

time: 119 us -> 119 us (level)
  no operation moved by 1% of the time
where the time goes in v6:
time: 119 us
  Pallas kernels  118 us (99%)
  between operations  1.29 us (1%)
    pallas_call x1, Pallas kernels, body(): pl.pallas_call(functools.partial(kernel, own_n, rep_n, cap), out_shape=(p...  114 us
    pallas_call x1, Pallas kernels, body(): pl.pallas_call(write_out, out_shape=tuple((jax.ShapeDtypeStruct(x.shape,...  3.66 us

profile of v6, /device:TPU:1, one launch (start us, length us, event | category | flops | bytes accessed | tf_op | source)
XLA Modules:
  0.0 119.1 jit_solution(10473849681646116574)
XLA Ops:
  1.3 114.1 %latent_code.1 = (bf16[1,1,32,8,18432]{4,3,2,1,0:T(8,128)(2,1)S(1)}, f32[1,288]{1,0:T(1,128)S(1)}, f32[1,288]{1,0:T(1,128)S(1)}) custom-call(s32[1]{0:T(128)S(6)} %copy.7.live_ref, s32[1,32]{1,0:T(1,128)} %bitcast.2, s32[1,32]{1,0:T(1,128)} %bitcast.3, bf16[64,64,576]{2,1,0:T(8,128)(2,1)} %pool_ref.1), custom_call_target="tpu_custom_call" | custom-call | tf_op jit(solution)/shard_map/latent_code/pallas_call | solution.py:390
  115.4 3.7 %write_out.1 = (bf16[1,1,32,8,18432]{4,3,2,1,0:T(8,128)(2,1)}, f32[1,288]{1,0:T(1,128)}, f32[1,288]{1,0:T(1,128)}) custom-call(bf16[1,1,32,8,18432]{4,3,2,1,0:T(8,128)(2,1)S(1)} %get-tuple-element.6.codes_v, f32[1,288]{1,0:T(1,128)S(1)} %get-tuple-element.7.steps_v, f32[1,288]{1,0:T(1,128)S(1)} %get-tuple-element.8.err_v), custom_call_target="tpu_custom_call" | custom-call | tf_op jit(solution)/shard_map/write_out/pallas_call | solution.py:431

commit v7 on v6

--- a/solution.py
+++ b/solution.py
@@ -263,7 +263,7 @@
             x = source[src, :, pl.ds(at, period)].astype(jnp.float32)
             codes_ref[0, 0, src, :, pl.ds(at, period)] = jnp.clip(x * inv_wide, -127.0, 127.0).astype(codes_ref.dtype)
             return carry
-        lax.fori_loop(0, tokens // group, one, 0)
+        lax.fori_loop(0, tokens // group, one, 0, unroll=4)
 
     def encode_and_sum(source, src, total):
         def one(i, total):

time: 119 us -> 119 us (level)
  no operation moved by 1% of the time
where the time goes in v7:
time: 119 us
  Pallas kernels  118 us (99%)
  between operations  1.29 us (1%)
    pallas_call x1, Pallas kernels, body(): pl.pallas_call(functools.partial(kernel, own_n, rep_n, cap), out_shape=(p...  114 us
    pallas_call x1, Pallas kernels, body(): pl.pallas_call(write_out, out_shape=tuple((jax.ShapeDtypeStruct(x.shape,...  3.66 us

profile of v7, /device:TPU:1, one launch (start us, length us, event | category | flops | bytes accessed | tf_op | source)
XLA Modules:
  0.0 119.0 jit_solution(8922478242206050254)
XLA Ops:
  1.3 114.0 %latent_code.1 = (bf16[1,1,32,8,18432]{4,3,2,1,0:T(8,128)(2,1)S(1)}, f32[1,288]{1,0:T(1,128)S(1)}, f32[1,288]{1,0:T(1,128)S(1)}) custom-call(s32[1]{0:T(128)S(6)} %copy.7.live_ref, s32[1,32]{1,0:T(1,128)} %bitcast.2, s32[1,32]{1,0:T(1,128)} %bitcast.3, bf16[64,64,576]{2,1,0:T(8,128)(2,1)} %pool_ref.1), custom_call_target="tpu_custom_call" | custom-call | tf_op jit(solution)/shard_map/latent_code/pallas_call | solution.py:390
  115.3 3.7 %write_out.1 = (bf16[1,1,32,8,18432]{4,3,2,1,0:T(8,128)(2,1)}, f32[1,288]{1,0:T(1,128)}, f32[1,288]{1,0:T(1,128)}) custom-call(bf16[1,1,32,8,18432]{4,3,2,1,0:T(8,128)(2,1)S(1)} %get-tuple-element.6.codes_v, f32[1,288]{1,0:T(1,128)S(1)} %get-tuple-element.7.steps_v, f32[1,288]{1,0:T(1,128)S(1)} %get-tuple-element.8.err_v), custom_call_target="tpu_custom_call" | custom-call | tf_op jit(solution)/shard_map/write_out/pallas_call | solution.py:431
